TPU v7x, 512 devices: a whole 4x8x8 slice. The times are simulated.
512 devices in a mesh: grp: 16 (over y, core), mem: 32 (over x, z).
Axes of the slice: x: 4, y: 8, z: 8, core: 2. Of those that a mesh axis runs over, the one named last changes fastest.
Arguments:
- v_stack: bfloat16 [524288, 512], P(('grp', 'mem')), may hold values from -0.1875 to 0.1875
- u_stack: bfloat16 [524288, 512], P(('grp', 'mem')), may hold values from -0.25 to 0.25
- warm_start: bfloat16 [524288, 256], P(('grp', 'mem')), may hold values from -3 to 3
- observed: bfloat16 [524288, 256], P(('grp', 'mem')), may hold values from -12 to 12, as said below
- owners: int32 [512, 4], replicated, may hold values from 0 to 511, as said below
- tile_ranks: int32 [512, 4], P(('grp', 'mem')), may hold values from 8 to 128
Outputs:
- model: float32 [524288, 256], P(('grp', 'mem'))
- residual: bfloat16 [524288, 256], P(('grp', 'mem'))
Inputs may be any that keep to these rules, and one draw needn't show every extreme that they name: Writing d = g * 32 + m, owners[d, t] = ((g + a_t) mod 16) * 32 + (m + b_t) mod 32, where the offsets a_t differ over t, the offsets b_t differ over t, some slot has a_t = 15, some slot has a_t = 8, some slot has b_t = 31 and some slot has b_t = 16. `observed`: entries of one row block share a scale.
All inputs are finite; a program needn't handle non-finite values.
Results may differ from a plain program's by a relative error of at most 0.006.
Values may be sent and summed in bfloat16 or wider, within the bound.
No kernel may reach another device: no remote copies, remote signals or barrier semaphores. Data moves between devices by JAX's collectives and lax.ppermute only.
A program may use at most 64 MiB of HBM per device.

v0:
```python
import jax
import jax.numpy as jnp
from jax import lax
from jax.sharding import Mesh
from jax.sharding import PartitionSpec as P

ITERS = 2
GRP = ("grp_0", "grp_1")
MEM = ("mem_0", "mem_1")
GRP_MEM = ("grp_0", "grp_1", "mem_0", "mem_1")


def one_axis_at_a_time(x, axes):
    for axis in axes:
        x = lax.psum(x, axis)
    return x


def pack_panels(panels, targets, peers):
    placing = (targets[:, None] == jnp.arange(peers, dtype=jnp.int32)[None, :]).astype(jnp.bfloat16)
    return jnp.einsum("tk,trh->krh", placing, panels, preferred_element_type=jnp.float32).astype(
        jnp.bfloat16
    )


def unpack_panels(received, chosen):
    return jnp.einsum(
        "kt,krh->trh", chosen.astype(jnp.bfloat16), received, preferred_element_type=jnp.float32
    ).astype(jnp.bfloat16)


def cross_groups(panels, group_steps):
    peers = lax.axis_size(GRP)
    own_group = lax.axis_index(GRP)
    outgoing = pack_panels(panels, (own_group + group_steps) % peers, peers)
    received = lax.all_to_all(outgoing, GRP, split_axis=0, concat_axis=0, tiled=True)
    anchors = (
        jnp.arange(peers, dtype=jnp.int32)[:, None] + group_steps[None, :]
    ) % peers == own_group
    return unpack_panels(received, anchors)


def cross_members(panels, member_steps):
    peers = lax.axis_size(MEM)
    own_member = lax.axis_index(MEM)
    outgoing = pack_panels(panels, (own_member + member_steps) % peers, peers)
    received = lax.all_to_all(outgoing, MEM, split_axis=0, concat_axis=0, tiled=True)
    anchors = (
        jnp.arange(peers, dtype=jnp.int32)[:, None] + member_steps[None, :]
    ) % peers == own_member
    return unpack_panels(received, anchors)


def route_panels(panels, group_steps, member_steps):
    moved = cross_groups(panels, group_steps)
    return cross_members(moved, member_steps)


def on_device(v_stack, u_stack, warm_start, observed, owners, tile_ranks):
    group_count = lax.axis_size(GRP)
    member_count = lax.axis_size(MEM)
    slots_held = owners.shape[1]
    stack_width = v_stack.shape[1]
    rank_cap = stack_width // slots_held
    right_count = warm_start.shape[1]
    live_rows = (
        lax.broadcasted_iota(jnp.int32, (slots_held, rank_cap), 1) < tile_ranks[0][:, None]
    ).astype(jnp.float32)
    forward_groups = owners[0] // member_count % group_count
    forward_members = owners[0] % member_count
    backward_groups = (group_count - forward_groups) % group_count
    backward_members = (member_count - forward_members) % member_count

    def forward(field):
        panels = jnp.einsum("bk,bh->kh", v_stack, field, preferred_element_type=jnp.float32)
        panels = (panels.reshape(slots_held, rank_cap, right_count) * live_rows[:, :, None]).astype(
            jnp.bfloat16
        )
        arrived = route_panels(panels, forward_groups, forward_members)
        return jnp.dot(
            u_stack, arrived.reshape(stack_width, right_count), preferred_element_type=jnp.float32
        )

    def adjoint(field):
        panels = jnp.einsum("bk,bh->kh", u_stack, field, preferred_element_type=jnp.float32)
        panels = panels.reshape(slots_held, rank_cap, right_count).astype(jnp.bfloat16)
        returned = route_panels(panels, backward_groups, backward_members)
        masked = (returned * live_rows[:, :, None]).astype(jnp.bfloat16)
        return jnp.dot(
            v_stack, masked.reshape(stack_width, right_count), preferred_element_type=jnp.float32
        )

    model = warm_start.astype(jnp.float32)
    residual = forward(warm_start) - observed.astype(jnp.float32)
    entries = float(warm_start.shape[0] * right_count * group_count * member_count)

    def iterate(index, carry):
        model, residual = carry
        spread = one_axis_at_a_time(jnp.sum(jnp.abs(residual)), GRP_MEM)
        huber_scale = 1.345 * spread / entries + 1e-06
        weights = huber_scale / jnp.maximum(jnp.abs(residual), huber_scale)
        weighted = (weights * residual).astype(jnp.bfloat16)
        gradient = adjoint(weighted)
        grad_sum = one_axis_at_a_time(jnp.sum(gradient * gradient), GRP_MEM)
        image_dir = forward(gradient.astype(jnp.bfloat16))
        curve_sum = one_axis_at_a_time(jnp.sum(weights * image_dir * image_dir), GRP_MEM)
        step_size = grad_sum / (curve_sum + 1e-06)
        return (model - step_size * gradient, residual - step_size * image_dir)

    model, residual = lax.fori_loop(0, ITERS, iterate, (model, residual))
    return (model, residual.astype(jnp.bfloat16))


def solution(mesh):
    finer = Mesh(mesh.devices.reshape(8, 2, 4, 8), ("grp_0", "grp_1", "mem_0", "mem_1"))
    placed = (
        P(GRP_MEM, None),
        P(GRP_MEM, None),
        P(GRP_MEM, None),
        P(GRP_MEM, None),
        P(),
        P(GRP_MEM, None),
    )
    return jax.shard_map(
        on_device,
        mesh=finer,
        in_specs=placed,
        out_specs=(P(GRP_MEM, None), P(GRP_MEM, None)),
        check_vma=False,
    )
```

profile of v0, /device:TPU:8, one launch (start us, length us, event | category | flops | bytes accessed | tf_op | source)
XLA Modules:
  0.0 714.6 jit_solution(6937026796179106969)
XLA Ops:
  6.2 9.2 %all-to-all-start.4 = ((bf16[16,128,256]{2,1,0:T(8,128)(2,1)}), bf16[16,128,256]{2,1,0:T(8,128)(2,1)S(1)}, u32[]{:S(2)}, u32[]{:S(2)}) async-start(bf16[16,128,256]{2,1,0:T(8,128)(2,1)} %copy.53), calls=%async_computation.4 | async-start | bytes 2097152 | tf_op jit(solution)/shard_map/all_to_all | solution.py:36
  15.5 24.6 %all-to-all-done.4 = bf16[16,128,256]{2,1,0:T(8,128)(2,1)S(1)} async-done(((bf16[16,128,256]{2,1,0:T(8,128)(2,1)}), bf16[16,128,256]{2,1,0:T(8,128)(2,1)S(1)}, u32[]{:S(2)}, u32[]{:S(2)}) %all-to-all-start.4) | async-done | bytes 1048608 | tf_op jit(solution)/shard_map/all_to_all | solution.py:36
  43.9 11.6 %all-to-all-start.5 = ((bf16[32,128,256]{2,1,0:T(8,128)(2,1)}), bf16[32,128,256]{2,1,0:T(8,128)(2,1)S(1)}, u32[]{:S(2)}, u32[]{:S(2)}) async-start(bf16[32,128,256]{2,1,0:T(8,128)(2,1)} %copy.55), calls=%async_computation.5 | async-start | bytes 4194304 | tf_op jit(solution)/shard_map/all_to_all | solution.py:47
  58.9 47.2 %all-to-all-done.5 = bf16[32,128,256]{2,1,0:T(8,128)(2,1)S(1)} async-done(((bf16[32,128,256]{2,1,0:T(8,128)(2,1)}), bf16[32,128,256]{2,1,0:T(8,128)(2,1)S(1)}, u32[]{:S(2)}, u32[]{:S(2)}) %all-to-all-start.5) | async-done | bytes 2097184 | tf_op jit(solution)/shard_map/all_to_all | solution.py:47
  110.1 599.7 %while.16 = (s32[]{:T(128)}, f32[1024,256]{0,1:T(8,128)}, f32[1024,256]{0,1:T(8,128)}, s32[4]{0:T(128)S(1)}, s32[4]{0:T(128)S(1)}, /*index=5*/bf16[1024,512]{1,0...) while((s32[]{:T(128)}, f32[1024,256]{0,1:T(8,128)}, ...), condition=%wide.region_16.17_spmd.clone, body=%wide.region_0.16_spmd.clone.sunk | while | flops 1133779456 | bytes 70786008 | solution.py:110
  112.2 16.6 %psum.148 = f32[]{:T(128)} all-reduce(f32[]{:T(128)} %abs_reduce_fusion.2), channel_id=1, replica_groups=mesh['grp_0'=8,'grp_1'=2,'mem_0'=4,'mem_1'=8] {'grp_0'}, use_global_device_ids=true, to_apply=%region_2.2 | all-reduce | flops 1 | bytes 8 | tf_op jit(solution)/shard_map/while/body/eval_jaxpr/psum | solution.py:15
  131.9 9.2 %psum.150 = f32[]{:T(128)} all-reduce(f32[]{:T(128)} %psum.149), channel_id=1, replica_groups=mesh['grp_0'=8,'grp_1'=2,'mem_0'=4,'mem_1'=8] {'mem_0'}, use_global_device_ids=true, to_apply=%region_4.4 | all-reduce | flops 1 | bytes 8 | tf_op jit(solution)/shard_map/while/body/eval_jaxpr/psum | solution.py:15
  141.1 18.6 %psum.151 = f32[]{:T(128)} all-reduce(f32[]{:T(128)} %psum.150), channel_id=1, replica_groups=mesh['grp_0'=8,'grp_1'=2,'mem_0'=4,'mem_1'=8] {'mem_1'}, use_global_device_ids=true, to_apply=%region_5.5 | all-reduce | flops 1 | bytes 8 | tf_op jit(solution)/shard_map/while/body/eval_jaxpr/psum | solution.py:15
  170.6 24.7 %all-to-all-done = bf16[16,128,256]{2,1,0:T(8,128)(2,1)} async-done(((bf16[16,128,256]{2,1,0:T(8,128)(2,1)}), bf16[16,128,256]{2,1,0:T(8,128)(2,1)}, u32[]{:S(2)}, u32[]{:S(2)}) %all-to-all-start) | async-done | bytes 1048608 | tf_op jit(solution)/shard_map/while/body/eval_jaxpr/all_to_all | solution.py:36
  206.2 50.5 %all-to-all-done.1 = bf16[32,128,256]{2,1,0:T(8,128)(2,1)S(1)} async-done(((bf16[32,128,256]{2,1,0:T(8,128)(2,1)}), bf16[32,128,256]{2,1,0:T(8,128)(2,1)S(1)}, u32[]{:S(2)}, u32[]{:S(2)}) %all-to-all-start.1) | async-done | bytes 2097184 | tf_op jit(solution)/shard_map/while/body/eval_jaxpr/all_to_all | solution.py:47
  268.7 24.7 %all-to-all-done.2 = bf16[16,128,256]{2,1,0:T(8,128)(2,1)} async-done(((bf16[16,128,256]{2,1,0:T(8,128)(2,1)}), bf16[16,128,256]{2,1,0:T(8,128)(2,1)}, u32[]{:S(2)}, u32[]{:S(2)}) %all-to-all-start.2) | async-done | bytes 1048608 | tf_op jit(solution)/shard_map/while/body/eval_jaxpr/all_to_all | solution.py:36
  305.3 50.5 %all-to-all-done.3 = bf16[32,128,256]{2,1,0:T(8,128)(2,1)S(1)} async-done(((bf16[32,128,256]{2,1,0:T(8,128)(2,1)}), bf16[32,128,256]{2,1,0:T(8,128)(2,1)S(1)}, u32[]{:S(2)}, u32[]{:S(2)}) %all-to-all-start.3) | async-done | bytes 2097184 | tf_op jit(solution)/shard_map/while/body/eval_jaxpr/all_to_all | solution.py:47
  359.8 16.8 %all-reduce.8 = (f32[]{:T(128)}, f32[]{:T(128)}) all-reduce(f32[]{:T(128)} %get-tuple-element.315, f32[]{:T(128)} %get-tuple-element.316), channel_id=1, replica_groups=mesh['grp_0'=8,'grp_1'=2,'mem_0'=4,'mem_1'=8] {'grp_0'}, use_global_device_ids=true, to_apply=%region_7.7 | all-reduce | flops 2 | bytes 16 | tf_op jit(solution)/shard_map/while/body/eval_jaxpr/psum | solution.py:15
  379.7 9.5 %all-reduce.10 = (f32[]{:T(128)}, f32[]{:T(128)}) all-reduce(f32[]{:T(128)} %get-tuple-element.319, f32[]{:T(128)} %get-tuple-element.320), channel_id=1, replica_groups=mesh['grp_0'=8,'grp_1'=2,'mem_0'=4,'mem_1'=8] {'mem_0'}, use_global_device_ids=true, to_apply=%region_9.9 | all-reduce | flops 2 | bytes 16 | tf_op jit(solution)/shard_map/while/body/eval_jaxpr/psum | solution.py:15
  389.2 18.3 %all-reduce.11 = (f32[]{:T(128)}, f32[]{:T(128)}) all-reduce(f32[]{:T(128)} %get-tuple-element.321, f32[]{:T(128)} %get-tuple-element.322), channel_id=1, replica_groups=mesh['grp_0'=8,'grp_1'=2,'mem_0'=4,'mem_1'=8] {'mem_1'}, use_global_device_ids=true, to_apply=%region_10.10 | all-reduce | flops 2 | bytes 16 | tf_op jit(solution)/shard_map/while/body/eval_jaxpr/psum | solution.py:15
  414.2 14.8 %psum.148 = f32[]{:T(128)} all-reduce(f32[]{:T(128)} %abs_reduce_fusion.2), channel_id=1, replica_groups=mesh['grp_0'=8,'grp_1'=2,'mem_0'=4,'mem_1'=8] {'grp_0'}, use_global_device_ids=true, to_apply=%region_2.2 | all-reduce | flops 1 | bytes 8 | tf_op jit(solution)/shard_map/while/body/eval_jaxpr/psum | solution.py:15
  440.4 15.6 %psum.151 = f32[]{:T(128)} all-reduce(f32[]{:T(128)} %psum.150), channel_id=1, replica_groups=mesh['grp_0'=8,'grp_1'=2,'mem_0'=4,'mem_1'=8] {'mem_1'}, use_global_device_ids=true, to_apply=%region_5.5 | all-reduce | flops 1 | bytes 8 | tf_op jit(solution)/shard_map/while/body/eval_jaxpr/psum | solution.py:15
  467.6 24.7 %all-to-all-done = bf16[16,128,256]{2,1,0:T(8,128)(2,1)} async-done(((bf16[16,128,256]{2,1,0:T(8,128)(2,1)}), bf16[16,128,256]{2,1,0:T(8,128)(2,1)}, u32[]{:S(2)}, u32[]{:S(2)}) %all-to-all-start) | async-done | bytes 1048608 | tf_op jit(solution)/shard_map/while/body/eval_jaxpr/all_to_all | solution.py:36
  504.0 50.5 %all-to-all-done.1 = bf16[32,128,256]{2,1,0:T(8,128)(2,1)S(1)} async-done(((bf16[32,128,256]{2,1,0:T(8,128)(2,1)}), bf16[32,128,256]{2,1,0:T(8,128)(2,1)S(1)}, u32[]{:S(2)}, u32[]{:S(2)}) %all-to-all-start.1) | async-done | bytes 2097184 | tf_op jit(solution)/shard_map/while/body/eval_jaxpr/all_to_all | solution.py:47
  566.4 24.7 %all-to-all-done.2 = bf16[16,128,256]{2,1,0:T(8,128)(2,1)} async-done(((bf16[16,128,256]{2,1,0:T(8,128)(2,1)}), bf16[16,128,256]{2,1,0:T(8,128)(2,1)}, u32[]{:S(2)}, u32[]{:S(2)}) %all-to-all-start.2) | async-done | bytes 1048608 | tf_op jit(solution)/shard_map/while/body/eval_jaxpr/all_to_all | solution.py:36
  603.0 50.5 %all-to-all-done.3 = bf16[32,128,256]{2,1,0:T(8,128)(2,1)S(1)} async-done(((bf16[32,128,256]{2,1,0:T(8,128)(2,1)}), bf16[32,128,256]{2,1,0:T(8,128)(2,1)S(1)}, u32[]{:S(2)}, u32[]{:S(2)}) %all-to-all-start.3) | async-done | bytes 2097184 | tf_op jit(solution)/shard_map/while/body/eval_jaxpr/all_to_all | solution.py:47
  657.6 16.8 %all-reduce.8 = (f32[]{:T(128)}, f32[]{:T(128)}) all-reduce(f32[]{:T(128)} %get-tuple-element.315, f32[]{:T(128)} %get-tuple-element.316), channel_id=1, replica_groups=mesh['grp_0'=8,'grp_1'=2,'mem_0'=4,'mem_1'=8] {'grp_0'}, use_global_device_ids=true, to_apply=%region_7.7 | all-reduce | flops 2 | bytes 16 | tf_op jit(solution)/shard_map/while/body/eval_jaxpr/psum | solution.py:15
  677.4 9.5 %all-reduce.10 = (f32[]{:T(128)}, f32[]{:T(128)}) all-reduce(f32[]{:T(128)} %get-tuple-element.319, f32[]{:T(128)} %get-tuple-element.320), channel_id=1, replica_groups=mesh['grp_0'=8,'grp_1'=2,'mem_0'=4,'mem_1'=8] {'mem_0'}, use_global_device_ids=true, to_apply=%region_9.9 | all-reduce | flops 2 | bytes 16 | tf_op jit(solution)/shard_map/while/body/eval_jaxpr/psum | solution.py:15
  687.0 18.3 %all-reduce.11 = (f32[]{:T(128)}, f32[]{:T(128)}) all-reduce(f32[]{:T(128)} %get-tuple-element.321, f32[]{:T(128)} %get-tuple-element.322), channel_id=1, replica_groups=mesh['grp_0'=8,'grp_1'=2,'mem_0'=4,'mem_1'=8] {'mem_1'}, use_global_device_ids=true, to_apply=%region_10.10 | all-reduce | flops 2 | bytes 16 | tf_op jit(solution)/shard_map/while/body/eval_jaxpr/psum | solution.py:15
  (95 shorter events, 152.4 us)
Async XLA Ops:
  6.2 33.9 %all-to-all-start.4 = ((bf16[16,128,256]{2,1,0:T(8,128)(2,1)}), bf16[16,128,256]{2,1,0:T(8,128)(2,1)S(1)}, u32[]{:S(2)}, u32[]{:S(2)}) async-start(bf16[16,128,256]{2,1,0:T(8,128)(2,1)} %copy.53), calls=%async_computation.4 | async-start | bytes 2097152 | tf_op jit(solution)/shard_map/all_to_all | solution.py:36
  43.9 11.6 %copy-start.3 = (bf16[1024,256]{1,0:T(8,128)(2,1)S(1)}, bf16[1024,256]{1,0:T(8,128)(2,1)}, u32[]{:S(2)}) copy-start(bf16[1024,256]{1,0:T(8,128)(2,1)} %param.10) | copy-start | bytes 1572868
  43.9 62.1 %all-to-all-start.5 = ((bf16[32,128,256]{2,1,0:T(8,128)(2,1)}), bf16[32,128,256]{2,1,0:T(8,128)(2,1)S(1)}, u32[]{:S(2)}, u32[]{:S(2)}) async-start(bf16[32,128,256]{2,1,0:T(8,128)(2,1)} %copy.55), calls=%async_computation.5 | async-start | bytes 4194304 | tf_op jit(solution)/shard_map/all_to_all | solution.py:47
  106.0 1.3 copy-start.2
  107.3 2.8 copy-start
  107.3 2.8 copy-start.4
  164.6 30.8 %all-to-all-start = ((bf16[16,128,256]{2,1,0:T(8,128)(2,1)}), bf16[16,128,256]{2,1,0:T(8,128)(2,1)}, u32[]{:S(2)}, u32[]{:S(2)}) async-start(bf16[16,128,256]{2,1,0:T(8,128)(2,1)} %copy.115), calls=%async_computation | async-start | bytes 2097152 | tf_op jit(solution)/shard_map/while/body/eval_jaxpr/all_to_all | solution.py:36
  200.3 56.4 %all-to-all-start.1 = ((bf16[32,128,256]{2,1,0:T(8,128)(2,1)}), bf16[32,128,256]{2,1,0:T(8,128)(2,1)S(1)}, u32[]{:S(2)}, u32[]{:S(2)}) async-start(bf16[32,128,256]{2,1,0:T(8,128)(2,1)} %copy.116), calls=%async_computation.1 | async-start | bytes 4194304 | tf_op jit(solution)/shard_map/while/body/eval_jaxpr/all_to_all | solution.py:47
  262.1 31.3 %all-to-all-start.2 = ((bf16[16,128,256]{2,1,0:T(8,128)(2,1)}), bf16[16,128,256]{2,1,0:T(8,128)(2,1)}, u32[]{:S(2)}, u32[]{:S(2)}) async-start(bf16[16,128,256]{2,1,0:T(8,128)(2,1)} %copy.119), calls=%async_computation.2 | async-start | bytes 2097152 | tf_op jit(solution)/shard_map/while/body/eval_jaxpr/all_to_all | solution.py:36
  298.4 57.4 %all-to-all-start.3 = ((bf16[32,128,256]{2,1,0:T(8,128)(2,1)}), bf16[32,128,256]{2,1,0:T(8,128)(2,1)S(1)}, u32[]{:S(2)}, u32[]{:S(2)}) async-start(bf16[32,128,256]{2,1,0:T(8,128)(2,1)} %copy.120), calls=%async_computation.3 | async-start | bytes 4194304 | tf_op jit(solution)/shard_map/while/body/eval_jaxpr/all_to_all | solution.py:47
  408.7 3.4 copy-start.1
  461.0 31.4 %all-to-all-start = ((bf16[16,128,256]{2,1,0:T(8,128)(2,1)}), bf16[16,128,256]{2,1,0:T(8,128)(2,1)}, u32[]{:S(2)}, u32[]{:S(2)}) async-start(bf16[16,128,256]{2,1,0:T(8,128)(2,1)} %copy.115), calls=%async_computation | async-start | bytes 2097152 | tf_op jit(solution)/shard_map/while/body/eval_jaxpr/all_to_all | solution.py:36
  497.3 57.1 %all-to-all-start.1 = ((bf16[32,128,256]{2,1,0:T(8,128)(2,1)}), bf16[32,128,256]{2,1,0:T(8,128)(2,1)S(1)}, u32[]{:S(2)}, u32[]{:S(2)}) async-start(bf16[32,128,256]{2,1,0:T(8,128)(2,1)} %copy.116), calls=%async_computation.1 | async-start | bytes 4194304 | tf_op jit(solution)/shard_map/while/body/eval_jaxpr/all_to_all | solution.py:47
  559.8 31.3 %all-to-all-start.2 = ((bf16[16,128,256]{2,1,0:T(8,128)(2,1)}), bf16[16,128,256]{2,1,0:T(8,128)(2,1)}, u32[]{:S(2)}, u32[]{:S(2)}) async-start(bf16[16,128,256]{2,1,0:T(8,128)(2,1)} %copy.119), calls=%async_computation.2 | async-start | bytes 2097152 | tf_op jit(solution)/shard_map/while/body/eval_jaxpr/all_to_all | solution.py:36
  596.1 57.4 %all-to-all-start.3 = ((bf16[32,128,256]{2,1,0:T(8,128)(2,1)}), bf16[32,128,256]{2,1,0:T(8,128)(2,1)S(1)}, u32[]{:S(2)}, u32[]{:S(2)}) async-start(bf16[32,128,256]{2,1,0:T(8,128)(2,1)} %copy.120), calls=%async_computation.3 | async-start | bytes 4194304 | tf_op jit(solution)/shard_map/while/body/eval_jaxpr/all_to_all | solution.py:47
  706.5 3.4 copy-start.1
where the time goes:
time: 716 us; the launch traced here: 715 us
  waiting for transfers between devices  373 us (52%)
  blocking collectives  185 us (26%)
  starting transfers between devices  72.9 us (10%)
  matrix products  38.4 us (5%)
  local copies, waits for them, and re-layouts  27.6 us (4%)
  other arithmetic  13.7 us (2%)
    all_to_all x5, waiting for transfers between devices, cross_members(): lax.all_to_all(outgoing, MEM, split_axis=0, concat_axis=0, tiled=True)  249 us
    psum x16, blocking collectives, one_axis_at_a_time(): x = lax.psum(x, axis)  185 us
    all_to_all x5, waiting for transfers between devices, cross_groups(): lax.all_to_all(outgoing, GRP, split_axis=0, concat_axis=0, tiled=True)  123 us
    all_to_all x5, starting transfers between devices, cross_members(): lax.all_to_all(outgoing, MEM, split_axis=0, concat_axis=0, tiled=True)  37.8 us
    all_to_all x5, starting transfers between devices, cross_groups(): lax.all_to_all(outgoing, GRP, split_axis=0, concat_axis=0, tiled=True)  35.1 us
    convert_element_type x10, local copies, waits for them, and re-layouts, pack_panels(): jnp.einsum('tk,trh->krh', placing, panels, preferred_element_type=jnp.flo...  19.5 us
    dot_general x10, matrix products, pack_panels(): jnp.einsum('tk,trh->krh', placing, panels, preferred_element_type=jnp.flo...  15 us
  transfers between devices with their start and end apart: 10, of which 10 were waited for; matrix products, arithmetic and copies ran while one was open for 0% of the time, Pallas kernels for 0%

commit v1 on v0

--- a/solution.py
+++ b/solution.py
@@ -12,7 +12,7 @@
 
 def one_axis_at_a_time(x, axes):
     for axis in axes:
-        x = lax.psum(x, axis)
+        x = jnp.sum(lax.all_gather(x, axis), axis=0)
     return x
 
 

time: 716 us -> 762 us (1.064)
  local copies, waits for them, and re-layouts: 27.6 us -> 70.7 us
  other arithmetic: 13.7 us -> 28.1 us
  blocking collectives: 185 us -> 174 us
    psum x16 -> x0, blocking collectives: 185 us -> none  [one_axis_at_a_time(): x = lax.psum(x, axis)]
    while x0 -> x16, blocking collectives: none -> 174 us
    while x4 -> x60, local copies, waits for them, and re-layouts: 0.01 us -> 43.3 us
    reduce_sum x0 -> x24, other arithmetic: none -> 14.4 us  [one_axis_at_a_time(): x = jnp.sum(lax.all_gather(x, axis), axis=0)]
  transfers between devices with their start and end apart: 10 -> 10, of which waited for: 10 -> 10; matrix products, arithmetic and copies ran while one was open for 0% -> 1% of each run, Pallas kernels for 0% -> 0%
where the time goes in v1:
time: 762 us; the launch traced here: 759 us
  waiting for transfers between devices  370 us (49%)
  blocking collectives  174 us (23%)
  starting transfers between devices  72.9 us (10%)
  local copies, waits for them, and re-layouts  70.7 us (9%)
  matrix products  38.4 us (5%)
  other arithmetic  28.1 us (4%)
    all_to_all x5, waiting for transfers between devices, cross_members(): lax.all_to_all(outgoing, MEM, split_axis=0, concat_axis=0, tiled=True)  246 us
    while x16, blocking collectives  174 us
    all_to_all x5, waiting for transfers between devices, cross_groups(): lax.all_to_all(outgoing, GRP, split_axis=0, concat_axis=0, tiled=True)  123 us
    while x60, local copies, waits for them, and re-layouts  43.3 us
    all_to_all x5, starting transfers between devices, cross_members(): lax.all_to_all(outgoing, MEM, split_axis=0, concat_axis=0, tiled=True)  37.8 us
    all_to_all x5, starting transfers between devices, cross_groups(): lax.all_to_all(outgoing, GRP, split_axis=0, concat_axis=0, tiled=True)  35.1 us
    convert_element_type x10, local copies, waits for them, and re-layouts, pack_panels(): jnp.einsum('tk,trh->krh', placing, panels, preferred_element_type=jnp.flo...  19.2 us
  transfers between devices with their start and end apart: 10, of which 10 were waited for; matrix products, arithmetic and copies ran while one was open for 1% of the time, Pallas kernels for 0%

profile of v1, /device:TPU:8, one launch (start us, length us, event | category | flops | bytes accessed | tf_op | source)
XLA Modules:
  0.0 759.1 jit_solution(11854337578516530302)
XLA Ops:
  6.2 9.2 %all-to-all-start.4 = ((bf16[16,128,256]{2,1,0:T(8,128)(2,1)}), bf16[16,128,256]{2,1,0:T(8,128)(2,1)S(1)}, u32[]{:S(2)}, u32[]{:S(2)}) async-start(bf16[16,128,256]{2,1,0:T(8,128)(2,1)} %copy.53), calls=%async_computation.4 | async-start | bytes 2097152 | tf_op jit(solution)/shard_map/all_to_all | solution.py:36
  15.5 24.6 %all-to-all-done.4 = bf16[16,128,256]{2,1,0:T(8,128)(2,1)S(1)} async-done(((bf16[16,128,256]{2,1,0:T(8,128)(2,1)}), bf16[16,128,256]{2,1,0:T(8,128)(2,1)S(1)}, u32[]{:S(2)}, u32[]{:S(2)}) %all-to-all-start.4) | async-done | bytes 1048608 | tf_op jit(solution)/shard_map/all_to_all | solution.py:36
  43.9 11.6 %all-to-all-start.5 = ((bf16[32,128,256]{2,1,0:T(8,128)(2,1)}), bf16[32,128,256]{2,1,0:T(8,128)(2,1)S(1)}, u32[]{:S(2)}, u32[]{:S(2)}) async-start(bf16[32,128,256]{2,1,0:T(8,128)(2,1)} %copy.55), calls=%async_computation.5 | async-start | bytes 4194304 | tf_op jit(solution)/shard_map/all_to_all | solution.py:47
  58.9 47.2 %all-to-all-done.5 = bf16[32,128,256]{2,1,0:T(8,128)(2,1)S(1)} async-done(((bf16[32,128,256]{2,1,0:T(8,128)(2,1)}), bf16[32,128,256]{2,1,0:T(8,128)(2,1)S(1)}, u32[]{:S(2)}, u32[]{:S(2)}) %all-to-all-start.5) | async-done | bytes 2097184 | tf_op jit(solution)/shard_map/all_to_all | solution.py:47
  110.1 644.2 %while.16 = (s32[]{:T(128)}, f32[1024,256]{0,1:T(8,128)}, f32[1024,256]{0,1:T(8,128)}, s32[4]{0:T(128)S(1)}, s32[4]{0:T(128)S(1)}, /*index=5*/bf16[1024,512]{1,0...) while((s32[]{:T(128)}, f32[1024,256]{0,1:T(8,128)}, ...), condition=%wide.region_16.17_spmd.clone, body=%wide.region_0.16_spmd.clone.sunk | while | flops 1133779456 | bytes 70787368 | solution.py:110
  114.9 15.9 %all-reduce.36 = f32[8]{0:T(128)S(1)} all-reduce(f32[8]{0:T(128)S(1)} %dynamic-update-slice.36), channel_id=1, replica_groups=mesh['grp_0'=8,'grp_1'=2,'mem_0'=4,'mem_1'=8] {'grp_0'}, use_global_device_ids=true, to_apply=%add | all-reduce | flops 8 | bytes 64 | tf_op jit(solution)/shard_map/while
  139.8 8.5 %all-reduce.38 = f32[4]{0:T(128)S(1)} all-reduce(f32[4]{0:T(128)S(1)} %dynamic-update-slice.38), channel_id=1, replica_groups=mesh['grp_0'=8,'grp_1'=2,'mem_0'=4,'mem_1'=8] {'mem_0'}, use_global_device_ids=true, to_apply=%add.2 | all-reduce | flops 4 | bytes 32 | tf_op jit(solution)/shard_map/while
  151.6 17.9 %all-reduce.39 = f32[8]{0:T(128)S(1)} all-reduce(f32[8]{0:T(128)S(1)} %dynamic-update-slice.39), channel_id=1, replica_groups=mesh['grp_0'=8,'grp_1'=2,'mem_0'=4,'mem_1'=8] {'mem_1'}, use_global_device_ids=true, to_apply=%add.3 | all-reduce | flops 8 | bytes 64 | tf_op jit(solution)/shard_map/while
  181.1 24.7 %all-to-all-done = bf16[16,128,256]{2,1,0:T(8,128)(2,1)} async-done(((bf16[16,128,256]{2,1,0:T(8,128)(2,1)}), bf16[16,128,256]{2,1,0:T(8,128)(2,1)}, u32[]{:S(2)}, u32[]{:S(2)}) %all-to-all-start) | async-done | bytes 1048608 | tf_op jit(solution)/shard_map/while/body/eval_jaxpr/all_to_all | solution.py:36
  216.7 50.5 %all-to-all-done.1 = bf16[32,128,256]{2,1,0:T(8,128)(2,1)S(1)} async-done(((bf16[32,128,256]{2,1,0:T(8,128)(2,1)}), bf16[32,128,256]{2,1,0:T(8,128)(2,1)S(1)}, u32[]{:S(2)}, u32[]{:S(2)}) %all-to-all-start.1) | async-done | bytes 2097184 | tf_op jit(solution)/shard_map/while/body/eval_jaxpr/all_to_all | solution.py:47
  279.1 24.7 %all-to-all-done.2 = bf16[16,128,256]{2,1,0:T(8,128)(2,1)} async-done(((bf16[16,128,256]{2,1,0:T(8,128)(2,1)}), bf16[16,128,256]{2,1,0:T(8,128)(2,1)}, u32[]{:S(2)}, u32[]{:S(2)}) %all-to-all-start.2) | async-done | bytes 1048608 | tf_op jit(solution)/shard_map/while/body/eval_jaxpr/all_to_all | solution.py:36
  317.1 49.2 %all-to-all-done.3 = bf16[32,128,256]{2,1,0:T(8,128)(2,1)S(1)} async-done(((bf16[32,128,256]{2,1,0:T(8,128)(2,1)}), bf16[32,128,256]{2,1,0:T(8,128)(2,1)S(1)}, u32[]{:S(2)}, u32[]{:S(2)}) %all-to-all-start.3) | async-done | bytes 2097184 | tf_op jit(solution)/shard_map/while/body/eval_jaxpr/all_to_all | solution.py:47
  371.6 16.1 %all-reduce.40 = (f32[8]{0:T(128)S(1)}, f32[8]{0:T(128)S(1)}) all-reduce(f32[8]{0:T(128)S(1)} %dynamic-update-slice.40, f32[8]{0:T(128)S(1)} %dynamic-update-slice.41), channel_id=1, replica_groups=mesh['grp_0'=8,'grp_1'=2,'mem_0'=4,'mem_1'=8] {'grp_0'}, use_global_device_ids=true, to_apply=%add.4 | all-reduce | flops 16 | bytes 128 | tf_op jit(solution)/shard_map/while
  398.1 8.8 %all-reduce.42 = (f32[4]{0:T(128)S(1)}, f32[4]{0:T(128)S(1)}) all-reduce(f32[4]{0:T(128)S(1)} %dynamic-update-slice.44, f32[4]{0:T(128)S(1)} %dynamic-update-slice.45), channel_id=1, replica_groups=mesh['grp_0'=8,'grp_1'=2,'mem_0'=4,'mem_1'=8] {'mem_0'}, use_global_device_ids=true, to_apply=%add.6 | all-reduce | flops 8 | bytes 64 | tf_op jit(solution)/shard_map/while
  410.9 17.7 %all-reduce.43 = (f32[8]{0:T(128)S(1)}, f32[8]{0:T(128)S(1)}) all-reduce(f32[8]{0:T(128)S(1)} %dynamic-update-slice.46, f32[8]{0:T(128)S(1)} %dynamic-update-slice.47), channel_id=1, replica_groups=mesh['grp_0'=8,'grp_1'=2,'mem_0'=4,'mem_1'=8] {'mem_1'}, use_global_device_ids=true, to_apply=%add.7 | all-reduce | flops 16 | bytes 128 | tf_op jit(solution)/shard_map/while
  439.1 14.1 %all-reduce.36 = f32[8]{0:T(128)S(1)} all-reduce(f32[8]{0:T(128)S(1)} %dynamic-update-slice.36), channel_id=1, replica_groups=mesh['grp_0'=8,'grp_1'=2,'mem_0'=4,'mem_1'=8] {'grp_0'}, use_global_device_ids=true, to_apply=%add | all-reduce | flops 8 | bytes 64 | tf_op jit(solution)/shard_map/while
  473.3 14.9 %all-reduce.39 = f32[8]{0:T(128)S(1)} all-reduce(f32[8]{0:T(128)S(1)} %dynamic-update-slice.39), channel_id=1, replica_groups=mesh['grp_0'=8,'grp_1'=2,'mem_0'=4,'mem_1'=8] {'mem_1'}, use_global_device_ids=true, to_apply=%add.3 | all-reduce | flops 8 | bytes 64 | tf_op jit(solution)/shard_map/while
  500.3 24.7 %all-to-all-done = bf16[16,128,256]{2,1,0:T(8,128)(2,1)} async-done(((bf16[16,128,256]{2,1,0:T(8,128)(2,1)}), bf16[16,128,256]{2,1,0:T(8,128)(2,1)}, u32[]{:S(2)}, u32[]{:S(2)}) %all-to-all-start) | async-done | bytes 1048608 | tf_op jit(solution)/shard_map/while/body/eval_jaxpr/all_to_all | solution.py:36
  536.7 50.5 %all-to-all-done.1 = bf16[32,128,256]{2,1,0:T(8,128)(2,1)S(1)} async-done(((bf16[32,128,256]{2,1,0:T(8,128)(2,1)}), bf16[32,128,256]{2,1,0:T(8,128)(2,1)S(1)}, u32[]{:S(2)}, u32[]{:S(2)}) %all-to-all-start.1) | async-done | bytes 2097184 | tf_op jit(solution)/shard_map/while/body/eval_jaxpr/all_to_all | solution.py:47
  599.1 24.7 %all-to-all-done.2 = bf16[16,128,256]{2,1,0:T(8,128)(2,1)} async-done(((bf16[16,128,256]{2,1,0:T(8,128)(2,1)}), bf16[16,128,256]{2,1,0:T(8,128)(2,1)}, u32[]{:S(2)}, u32[]{:S(2)}) %all-to-all-start.2) | async-done | bytes 1048608 | tf_op jit(solution)/shard_map/while/body/eval_jaxpr/all_to_all | solution.py:36
  637.1 49.2 %all-to-all-done.3 = bf16[32,128,256]{2,1,0:T(8,128)(2,1)S(1)} async-done(((bf16[32,128,256]{2,1,0:T(8,128)(2,1)}), bf16[32,128,256]{2,1,0:T(8,128)(2,1)S(1)}, u32[]{:S(2)}, u32[]{:S(2)}) %all-to-all-start.3) | async-done | bytes 2097184 | tf_op jit(solution)/shard_map/while/body/eval_jaxpr/all_to_all | solution.py:47
  691.6 16.1 %all-reduce.40 = (f32[8]{0:T(128)S(1)}, f32[8]{0:T(128)S(1)}) all-reduce(f32[8]{0:T(128)S(1)} %dynamic-update-slice.40, f32[8]{0:T(128)S(1)} %dynamic-update-slice.41), channel_id=1, replica_groups=mesh['grp_0'=8,'grp_1'=2,'mem_0'=4,'mem_1'=8] {'grp_0'}, use_global_device_ids=true, to_apply=%add.4 | all-reduce | flops 16 | bytes 128 | tf_op jit(solution)/shard_map/while
  718.1 8.8 %all-reduce.42 = (f32[4]{0:T(128)S(1)}, f32[4]{0:T(128)S(1)}) all-reduce(f32[4]{0:T(128)S(1)} %dynamic-update-slice.44, f32[4]{0:T(128)S(1)} %dynamic-update-slice.45), channel_id=1, replica_groups=mesh['grp_0'=8,'grp_1'=2,'mem_0'=4,'mem_1'=8] {'mem_0'}, use_global_device_ids=true, to_apply=%add.6 | all-reduce | flops 8 | bytes 64 | tf_op jit(solution)/shard_map/while
  730.8 17.7 %all-reduce.43 = (f32[8]{0:T(128)S(1)}, f32[8]{0:T(128)S(1)}) all-reduce(f32[8]{0:T(128)S(1)} %dynamic-update-slice.46, f32[8]{0:T(128)S(1)} %dynamic-update-slice.47), channel_id=1, replica_groups=mesh['grp_0'=8,'grp_1'=2,'mem_0'=4,'mem_1'=8] {'mem_1'}, use_global_device_ids=true, to_apply=%add.7 | all-reduce | flops 16 | bytes 128 | tf_op jit(solution)/shard_map/while
  (175 shorter events, 206.8 us)
Async XLA Ops:
  6.2 33.9 %all-to-all-start.4 = ((bf16[16,128,256]{2,1,0:T(8,128)(2,1)}), bf16[16,128,256]{2,1,0:T(8,128)(2,1)S(1)}, u32[]{:S(2)}, u32[]{:S(2)}) async-start(bf16[16,128,256]{2,1,0:T(8,128)(2,1)} %copy.53), calls=%async_computation.4 | async-start | bytes 2097152 | tf_op jit(solution)/shard_map/all_to_all | solution.py:36
  43.9 11.6 %copy-start.3 = (bf16[1024,256]{1,0:T(8,128)(2,1)S(1)}, bf16[1024,256]{1,0:T(8,128)(2,1)}, u32[]{:S(2)}) copy-start(bf16[1024,256]{1,0:T(8,128)(2,1)} %param.10) | copy-start | bytes 1572868
  43.9 62.1 %all-to-all-start.5 = ((bf16[32,128,256]{2,1,0:T(8,128)(2,1)}), bf16[32,128,256]{2,1,0:T(8,128)(2,1)S(1)}, u32[]{:S(2)}, u32[]{:S(2)}) async-start(bf16[32,128,256]{2,1,0:T(8,128)(2,1)} %copy.55), calls=%async_computation.5 | async-start | bytes 4194304 | tf_op jit(solution)/shard_map/all_to_all | solution.py:47
  106.0 1.3 copy-start.2
  107.3 2.8 copy-start
  107.3 2.8 copy-start.4
  175.0 30.8 %all-to-all-start = ((bf16[16,128,256]{2,1,0:T(8,128)(2,1)}), bf16[16,128,256]{2,1,0:T(8,128)(2,1)}, u32[]{:S(2)}, u32[]{:S(2)}) async-start(bf16[16,128,256]{2,1,0:T(8,128)(2,1)} %copy.115), calls=%async_computation | async-start | bytes 2097152 | tf_op jit(solution)/shard_map/while/body/eval_jaxpr/all_to_all | solution.py:36
  210.8 56.4 %all-to-all-start.1 = ((bf16[32,128,256]{2,1,0:T(8,128)(2,1)}), bf16[32,128,256]{2,1,0:T(8,128)(2,1)S(1)}, u32[]{:S(2)}, u32[]{:S(2)}) async-start(bf16[32,128,256]{2,1,0:T(8,128)(2,1)} %copy.116), calls=%async_computation.1 | async-start | bytes 4194304 | tf_op jit(solution)/shard_map/while/body/eval_jaxpr/all_to_all | solution.py:47
  272.5 31.3 %all-to-all-start.2 = ((bf16[16,128,256]{2,1,0:T(8,128)(2,1)}), bf16[16,128,256]{2,1,0:T(8,128)(2,1)}, u32[]{:S(2)}, u32[]{:S(2)}) async-start(bf16[16,128,256]{2,1,0:T(8,128)(2,1)} %copy.119), calls=%async_computation.2 | async-start | bytes 2097152 | tf_op jit(solution)/shard_map/while/body/eval_jaxpr/all_to_all | solution.py:36
  308.8 57.4 %all-to-all-start.3 = ((bf16[32,128,256]{2,1,0:T(8,128)(2,1)}), bf16[32,128,256]{2,1,0:T(8,128)(2,1)S(1)}, u32[]{:S(2)}, u32[]{:S(2)}) async-start(bf16[32,128,256]{2,1,0:T(8,128)(2,1)} %copy.120), calls=%async_computation.3 | async-start | bytes 4194304 | tf_op jit(solution)/shard_map/while/body/eval_jaxpr/all_to_all | solution.py:47
  431.0 3.4 copy-start.1
  493.7 31.4 %all-to-all-start = ((bf16[16,128,256]{2,1,0:T(8,128)(2,1)}), bf16[16,128,256]{2,1,0:T(8,128)(2,1)}, u32[]{:S(2)}, u32[]{:S(2)}) async-start(bf16[16,128,256]{2,1,0:T(8,128)(2,1)} %copy.115), calls=%async_computation | async-start | bytes 2097152 | tf_op jit(solution)/shard_map/while/body/eval_jaxpr/all_to_all | solution.py:36
  530.1 57.1 %all-to-all-start.1 = ((bf16[32,128,256]{2,1,0:T(8,128)(2,1)}), bf16[32,128,256]{2,1,0:T(8,128)(2,1)S(1)}, u32[]{:S(2)}, u32[]{:S(2)}) async-start(bf16[32,128,256]{2,1,0:T(8,128)(2,1)} %copy.116), calls=%async_computation.1 | async-start | bytes 4194304 | tf_op jit(solution)/shard_map/while/body/eval_jaxpr/all_to_all | solution.py:47
  592.5 31.3 %all-to-all-start.2 = ((bf16[16,128,256]{2,1,0:T(8,128)(2,1)}), bf16[16,128,256]{2,1,0:T(8,128)(2,1)}, u32[]{:S(2)}, u32[]{:S(2)}) async-start(bf16[16,128,256]{2,1,0:T(8,128)(2,1)} %copy.119), calls=%async_computation.2 | async-start | bytes 2097152 | tf_op jit(solution)/shard_map/while/body/eval_jaxpr/all_to_all | solution.py:36
  628.8 57.4 %all-to-all-start.3 = ((bf16[32,128,256]{2,1,0:T(8,128)(2,1)}), bf16[32,128,256]{2,1,0:T(8,128)(2,1)S(1)}, u32[]{:S(2)}, u32[]{:S(2)}) async-start(bf16[32,128,256]{2,1,0:T(8,128)(2,1)} %copy.120), calls=%async_computation.3 | async-start | bytes 4194304 | tf_op jit(solution)/shard_map/while/body/eval_jaxpr/all_to_all | solution.py:47
  751.0 3.4 copy-start.1
